TPU v7x, 32 devices: a whole 2x2x4 slice. The times are simulated.
32 devices in a mesh: win: 2 (over y), dx: 4 (over z), dy: 2 (over x), dz: 2 (over core).
Axes of the slice: x: 2, y: 2, z: 4, core: 2. Of those that a mesh axis runs over, the one named last changes fastest.
Arguments:
- fraction: float32 [3, 8, 2, 2, 768], P(None, ('win', 'dx'), 'dy', 'dz'), parts along dimension 1, may hold values from 0 to 1
- atom_type: int32 [8, 2, 2, 768], P(('win', 'dx'), 'dy', 'dz'), parts along dimension 0, may hold values from 0 to 31
- perturbed: int32 [8, 2, 2, 768], P(('win', 'dx'), 'dy', 'dz'), parts along dimension 0, may hold values from 0 to 1
- leaving: int32 [8, 2, 2, 2, 16], P(('win', 'dx'), 'dy', 'dz'), parts along dimension 0, may hold values from 0 to 767, as said below
- neighbours: int32 [8, 2, 2, 6, 16], P(('win', 'dx'), 'dy', 'dz'), parts along dimension 0, may hold values from 0 to 161, as said below
- counts: int32 [8, 2, 2, 6], P(('win', 'dx'), 'dy', 'dz'), parts along dimension 0, may hold values from 1 to 16, as said below
- sigma_table: float32 [32], replicated, may hold values from 0.8 to 1.2
- depth_table: float32 [32], replicated, may hold values from 0.002 to 0.03
- charge_table: float32 [32], replicated, may hold values from -1 to 1
- domain_edge: float32 [3], replicated, may hold values from 1 to 1.12
- coupling: float32 [2], P('win'), parts along dimension 0, may hold values from 0.1 to 0.9
Outputs:
- forces: float32 [3, 8, 2, 2, 768], P(None, ('win', 'dx'), 'dy', 'dz'), parts along dimension 1
- energy: float32 [2], P('win'), parts along dimension 0
- dhdl: float32 [2], P('win'), parts along dimension 0
There are 2 independent parts, one for each index of `win`. A program takes and returns all parts, laid end to end along the dimension named above; an argument that names none is the same for every part. Nothing has to cross between parts.
Inputs may be any that keep to these rules, and one draw needn't show every extreme that they name: `leaving`: each domain lists 2 * 16 distinct slots: the first 16 leave toward the next domain, the last 16 toward the previous one. `neighbours`: each list holds 16 distinct ghost block numbers; entries at or past the block's count are valid numbers and are not used. `counts`: some block lists exactly 16 blocks in every draw.
All inputs are finite; a program needn't handle non-finite values.
Results may differ from a plain program's by a relative error of at most 0.0003.
Values sent between devices are 32-bit elements; how exact they have to be, the bound alone decides.
A program may use at most 64 MiB of HBM per device.

v0:
```python
import jax
import jax.numpy as jnp
from jax import lax
from jax.sharding import PartitionSpec as P

soft_base = 0.3
soft_alpha = 0.5
charge_base = 0.3
charge_alpha = 0.5
coulomb = 0.1


def passed_along(array, axis, by):
    devices = lax.axis_size(axis)
    return lax.ppermute(array, axis, [(i, (i + by) % devices) for i in range(devices)])


def extended(block, sides, width):
    for axis, dim in sides:
        count = lax.axis_size(axis)
        forward = [(i, i + 1) for i in range(count - 1)]
        forward.append((count - 1, 0))
        backward = [(target, source) for source, target in forward]
        low = lax.ppermute(
            lax.slice_in_dim(block, block.shape[dim] - width, None, axis=dim), axis, forward
        )
        high = lax.ppermute(lax.slice_in_dim(block, 0, width, axis=dim), axis, backward)
        block = jnp.concatenate([low, block, high], axis=dim)
    return block


def swapped(block, axis, bit):
    count = lax.axis_size(axis)
    route = []
    for low in range(count):
        high = low | 1 << bit
        if high != low and high < count:
            route += [(low, high), (high, low)]
    return lax.ppermute(block, axis, route)


def lookup(table_row, type_ids):
    onehot = type_ids[None, :] == jnp.arange(table_row.shape[0], dtype=jnp.int32)[:, None]
    return jnp.sum(jnp.where(onehot, table_row[:, None], jnp.float32(0.0)), axis=0)


def pair_block(own_block, other_blocks, live_pairs, coupling_value):
    separation = own_block[0:3][None, :, :, None] - other_blocks[:, 0:3][:, :, None, :]
    radius_sq = jnp.sum(separation * separation, axis=1)
    sigma_pair = 0.5 * (own_block[3][None, :, None] + other_blocks[:, 3][:, None, :])
    depth_pair = jnp.sqrt(own_block[4][None, :, None] * other_blocks[:, 4][:, None, :])
    charges = own_block[5][None, :, None] * other_blocks[:, 5][:, None, :]
    flagged = jnp.maximum(own_block[6][None, :, None], other_blocks[:, 6][:, None, :])
    scaled = coupling_value * flagged
    sigma_two = sigma_pair * sigma_pair
    sigma_six = sigma_two * sigma_two * sigma_two
    soft_six = sigma_six * (soft_base + soft_alpha * scaled) + radius_sq * radius_sq * radius_sq
    soft_two = charge_base + charge_alpha * scaled + radius_sq
    inverse_six = 1.0 / soft_six
    energy_lj = (
        4.0
        * depth_pair
        * (sigma_six * sigma_six * inverse_six * inverse_six - sigma_six * inverse_six)
    )
    grad_six = (
        4.0
        * depth_pair
        * (
            sigma_six * inverse_six * inverse_six
            - 2.0 * sigma_six * sigma_six * inverse_six * inverse_six * inverse_six
        )
    )
    energy_coul = coulomb * charges * lax.rsqrt(soft_two)
    grad_two = -0.5 * energy_coul / soft_two
    weight = 1.0 - scaled
    total_pair = energy_lj + energy_coul
    pair_energy = jnp.sum(weight * total_pair * live_pairs)
    pair_dhdl = jnp.sum(
        flagged
        * (-total_pair + weight * (grad_six * sigma_six * soft_alpha + grad_two * charge_alpha))
        * live_pairs
    )
    force_scale = -weight * (6.0 * radius_sq * radius_sq * grad_six + 2.0 * grad_two) * live_pairs
    forces = jnp.sum(force_scale[:, None] * separation, axis=(0, 3))
    return (forces, pair_energy, pair_dhdl)


def block_terms(ghost_rows, listed_blocks, list_count, block_id, block_total, coupling_value):
    centre = 13 * block_total + block_id
    own_block = lax.dynamic_index_in_dim(ghost_rows, centre, 0, keepdims=False)
    other_blocks = jnp.take(ghost_rows, listed_blocks, axis=0)
    valid_slot = (jnp.arange(listed_blocks.shape[0], dtype=jnp.int32) < list_count).astype(
        jnp.float32
    )
    is_self = (listed_blocks == centre).astype(jnp.float32)[:, None, None] * jnp.eye(
        128, dtype=jnp.float32
    )[None]
    live_pairs = valid_slot[:, None, None] * (1.0 - is_self)
    return pair_block(own_block, other_blocks, live_pairs, coupling_value)


def on_device(
    fraction,
    atom_type,
    perturbed,
    leaving,
    neighbours,
    counts,
    sigma_table,
    depth_table,
    charge_table,
    domain_edge,
    coupling,
):
    atom_count = fraction.shape[-1]
    block_total = atom_count // 128
    spacing = float(atom_count) ** (1.0 / 3.0)
    type_ids = atom_type.reshape(atom_count)
    payload = jnp.concatenate(
        [
            fraction.reshape(3, atom_count),
            lookup(sigma_table, type_ids)[None],
            lookup(depth_table, type_ids)[None],
            lookup(charge_table, type_ids)[None],
            perturbed.reshape(1, atom_count).astype(jnp.float32),
        ],
        axis=0,
    )
    leave_slots = leaving.reshape(2, -1)
    shift_x = jnp.zeros((7, 1), jnp.float32).at[0].set(1.0)
    upward = payload[:, leave_slots[0]]
    downward = payload[:, leave_slots[1]]
    from_below = passed_along(upward, "dx", 1) - shift_x
    from_above = passed_along(downward, "dx", -1) + shift_x
    moved = payload.at[:, leave_slots[1]].set(from_below).at[:, leave_slots[0]].set(from_above)
    domain_block = moved.reshape(7, 1, 1, 1, atom_count)
    ghost_plane = extended(domain_block, (("dx", 1), ("dy", 2)), 1)
    partner = swapped(ghost_plane, "dz", 0)
    ghost_cells = jnp.concatenate([partner, ghost_plane, partner], axis=3)
    image_steps = jnp.arange(3, dtype=jnp.float32) - 1.0
    position = jnp.stack(
        [
            (ghost_cells[0] + image_steps[:, None, None, None]) * domain_edge[0] * spacing,
            (ghost_cells[1] + image_steps[None, :, None, None]) * domain_edge[1] * spacing,
            (ghost_cells[2] + image_steps[None, None, :, None]) * domain_edge[2] * spacing,
        ],
        axis=0,
    )
    ghost_all = jnp.concatenate([position, ghost_cells[3:]], axis=0)
    ghost_rows = (
        ghost_all.reshape(7, 27, block_total, 128)
        .transpose(1, 2, 0, 3)
        .reshape(27 * block_total, 7, 128)
    )
    listed = neighbours.reshape(block_total, -1)
    listed_count = counts.reshape(block_total)
    coupling_value = coupling[0]

    def one_block(block_id):
        return block_terms(
            ghost_rows,
            listed[block_id],
            listed_count[block_id],
            block_id,
            block_total,
            coupling_value,
        )

    forces, energies, dhdls = lax.map(one_block, jnp.arange(block_total, dtype=jnp.int32))
    forces = forces.transpose(1, 0, 2).reshape(3, 1, 1, 1, atom_count)
    window_energy, window_dhdl = lax.psum((jnp.sum(energies), jnp.sum(dhdls)), ("dx", "dy", "dz"))
    slot_total = jnp.float32(
        atom_count * lax.axis_size("dx") * lax.axis_size("dy") * lax.axis_size("dz")
    )
    energy = (0.5 * window_energy / slot_total).reshape(1)
    dhdl = (0.5 * window_dhdl / slot_total).reshape(1)
    return (forces, energy, dhdl)


def solution(mesh):
    return jax.shard_map(
        on_device,
        mesh=mesh,
        in_specs=(
            P(None, ("win", "dx"), "dy", "dz", None),
            P(("win", "dx"), "dy", "dz", None),
            P(("win", "dx"), "dy", "dz", None),
            P(("win", "dx"), "dy", "dz", None, None),
            P(("win", "dx"), "dy", "dz", None, None),
            P(("win", "dx"), "dy", "dz", None),
            P(),
            P(),
            P(),
            P(),
            P("win"),
        ),
        out_specs=(P(None, ("win", "dx"), "dy", "dz", None), P("win"), P("win")),
        check_vma=False,
    )
```

profile of v0, /device:TPU:0, one launch (start us, length us, event | category | flops | bytes accessed | tf_op | source)
XLA Modules:
  0.0 154.2 jit_solution(11909424343959024680)
XLA Ops:
  0.6 0.8 fusion.44
  1.4 0.7 convert_bitcast_fusion
  2.1 0.7 reduce.2
  2.8 0.8 select_reduce_fusion
  3.6 0.7 copy.79
  5.1 3.1 %collective-permute-start = (f32[7,16]{0,1:T(8,128)S(1)}, f32[7,16]{0,1:T(8,128)S(1)}, u32[]{:S(2)}, u32[]{:S(2)}) collective-permute-start(f32[7,16]{0,1:T(8,128)S(1)} %bitcast.113), channel_id=1, source_target_pairs={{0,4},{4,8},{8,12},{12,0},{1,5},{5,9},{9,13},{13,1},{2,6},{6,10},{... | collective-permute-start | bytes 1352 | tf_op jit(solution)/shard_map/ppermute | solution.py:15
  8.8 2.1 %collective-permute-start.1 = (f32[7,16]{0,1:T(8,128)S(1)}, f32[7,16]{0,1:T(8,128)S(1)}, u32[]{:S(2)}, u32[]{:S(2)}) collective-permute-start(f32[7,16]{0,1:T(8,128)S(1)} %bitcast.112), channel_id=1, source_target_pairs={{0,12},{4,0},{8,4},{12,8},{1,13},{5,1},{9,5},{13,9},{2,14},{6,2},{... | collective-permute-start | bytes 1352 | tf_op jit(solution)/shard_map/ppermute | solution.py:15
  10.9 1.0 collective-permute-done
  11.9 0.9 scatter_custom_fusion
  12.9 0.8 scatter_custom_fusion.1
  13.7 3.5 %collective-permute-start.3 = (f32[7,1,1,1,768]{0,4,3,2,1:T(8,128)S(1)}, f32[7,1,1,1,768]{0,4,3,2,1:T(8,128)S(1)}, u32[]{:S(2)}, u32[]{:S(2)}) collective-permute-start(f32[7,1,1,1,768]{0,4,3,2,1:T(8,128)S(1)} %bitcast.97), channel_id=1, source_target_pairs={{4,0},{8,4},{12,8},{0,12},{5,1},{9,5},{13,9},{1,13},{6,2},{10,6},{... | collective-permute-start | bytes 64520 | tf_op jit(solution)/shard_map/ppermute | solution.py:27
  17.4 9.4 %collective-permute-done.3 = f32[7,1,1,1,768]{0,4,3,2,1:T(8,128)S(1)} collective-permute-done((f32[7,1,1,1,768]{0,4,3,2,1:T(8,128)S(1)}, f32[7,1,1,1,768]{0,4,3,2,1:T(8,128)S(1)}, u32[]{:S(2)}, u32[]{:S(2)}) %collective-permute-start.3) | collective-permute-done | bytes 21536 | tf_op jit(solution)/shard_map/ppermute | solution.py:27
  26.9 6.7 %collective-permute-done.2 = f32[7,1,1,1,768]{0,4,3,2,1:T(8,128)S(1)} collective-permute-done((f32[7,1,1,1,768]{0,4,3,2,1:T(8,128)S(1)}, f32[7,1,1,1,768]{0,4,3,2,1:T(8,128)S(1)}, u32[]{:S(2)}, u32[]{:S(2)}) %collective-permute-start.2) | collective-permute-done | bytes 21536 | tf_op jit(solution)/shard_map/ppermute | solution.py:24
  33.9 1.6 %collective-permute-start.5 = (f32[7,3,1,1,768]{4,3,2,1,0:T(1,128)S(1)}, f32[7,3,1,1,768]{4,3,2,1,0:T(1,128)S(1)}, u32[]{:S(2)}, u32[]{:S(2)}) collective-permute-start(f32[7,3,1,1,768]{4,3,2,1,0:T(1,128)S(1)} %pad_maximum_fusion.2), channel_id=1, source_target_pairs={{2,0},{0,2},{3,1},{1,3},{6,4},{4,6},{7,5},{5,7},{10,8},{8,10},{11,... | collective-permute-start | bytes 193544 | tf_op jit(solution)/shard_map/ppermute | solution.py:27
  36.0 2.2 %collective-permute-done.5 = f32[7,3,1,1,768]{4,3,2,1,0:T(1,128)S(1)} collective-permute-done((f32[7,3,1,1,768]{4,3,2,1,0:T(1,128)S(1)}, f32[7,3,1,1,768]{4,3,2,1,0:T(1,128)S(1)}, u32[]{:S(2)}, u32[]{:S(2)}) %collective-permute-start.5) | collective-permute-done | bytes 64544 | tf_op jit(solution)/shard_map/ppermute | solution.py:27
  38.2 1.5 collective-permute-done.4
  39.9 0.7 fusion.46
  40.6 0.7 collective-permute-done.6
  41.5 2.3 %fusion.34 = (f32[1,3,3,3,768]{4,0,3,2,1:T(1,128)S(1)}, f32[1,3,3,3,768]{4,0,3,2,1:T(1,128)S(1)}, f32[1,3,3,3,768]{4,0,3,2,1:T(1,128)S(1)}) fusion(f32[7,3,3,3,768]{4,0,3,2,1:T(8,128)S(1)} %copy_dynamic-update-slice_fusion.1, f32[3]{0:T(128)S(1)} %iota_add_fusion, f32[]{:T(128)} %bitcast.28, f32[]{:T(128)} %bitcast.32, f32[]{:T(128)} %bitcast.30), kind=kLoop, calls=%fused_computation.81 | loop fusion | flops 186624 | bytes 499212 | tf_op jit(solution)/shard_map/mul | solution.py:143
  44.2 72.7 %while.17 = (s32[]{:T(128)}, f32[6,3,128]{2,1,0:T(4,128)S(1)}, f32[6]{0:T(128)S(1)}, f32[6]{0:T(128)S(1)}, f32[]{:T(128)}, /*index=5*/s32[6]{0:T(128)S(1)}, f32[...) while((s32[]{:T(128)}, f32[6,3,128]{2,1,0:T(4,128)S(1)}, ...), condition=%wide.region_10.11_spmd, body=%wide.region_5.10_spmd.sunk | while | flops 20495192 | bytes 4781457 | solution.py:169
  48.6 0.7 compare_convert_fusion.3
  50.5 3.8 %fusion.57 = (f32[]{:T(128)}, f32[]{:T(128)}, f32[16,128,128]{2,1,0:T(8,128)S(1)}) fusion(f32[128,128]{1,0:T(8,128)S(1)} %fusion.53, f32[16]{0:T(128)S(1)} %get-tuple-element.249, f32[16]{0:T(128)S(1)} %get-tuple-element.250, f32[16,128]{1,0:T(8,128)S(1)} %bitcast.104, f32[128]{0:T(128)S(1)} %get-tuple-element.253, f32[16,128]{1,0:T(8,128)S(1)} %bitcast.105, ...), kind=kLoop, calls=%fused_computation.33.clone.1 | loop fusion | flops 15990782 | bytes 2197644 | tf_op jit(solution)/shard_map/while/body/eval_jaxpr/reduce_sum | solution.py:78
  54.8 0.8 dynamic_update_slice.25
  55.6 0.8 dynamic_update_slice.26
  60.8 0.7 compare_convert_fusion.3
  62.6 3.8 %fusion.57 = (f32[]{:T(128)}, f32[]{:T(128)}, f32[16,128,128]{2,1,0:T(8,128)S(1)}) fusion(f32[128,128]{1,0:T(8,128)S(1)} %fusion.53, f32[16]{0:T(128)S(1)} %get-tuple-element.249, f32[16]{0:T(128)S(1)} %get-tuple-element.250, f32[16,128]{1,0:T(8,128)S(1)} %bitcast.104, f32[128]{0:T(128)S(1)} %get-tuple-element.253, f32[16,128]{1,0:T(8,128)S(1)} %bitcast.105, ...), kind=kLoop, calls=%fused_computation.33.clone.1 | loop fusion | flops 15990782 | bytes 2197644 | tf_op jit(solution)/shard_map/while/body/eval_jaxpr/reduce_sum | solution.py:78
  66.9 0.8 dynamic_update_slice.25
  67.7 0.8 dynamic_update_slice.26
  72.9 0.7 compare_convert_fusion.3
  74.7 3.8 %fusion.57 = (f32[]{:T(128)}, f32[]{:T(128)}, f32[16,128,128]{2,1,0:T(8,128)S(1)}) fusion(f32[128,128]{1,0:T(8,128)S(1)} %fusion.53, f32[16]{0:T(128)S(1)} %get-tuple-element.249, f32[16]{0:T(128)S(1)} %get-tuple-element.250, f32[16,128]{1,0:T(8,128)S(1)} %bitcast.104, f32[128]{0:T(128)S(1)} %get-tuple-element.253, f32[16,128]{1,0:T(8,128)S(1)} %bitcast.105, ...), kind=kLoop, calls=%fused_computation.33.clone.1 | loop fusion | flops 15990782 | bytes 2197644 | tf_op jit(solution)/shard_map/while/body/eval_jaxpr/reduce_sum | solution.py:78
  79.0 0.8 dynamic_update_slice.25
  79.8 0.8 dynamic_update_slice.26
  85.0 0.7 compare_convert_fusion.3
  86.8 3.8 %fusion.57 = (f32[]{:T(128)}, f32[]{:T(128)}, f32[16,128,128]{2,1,0:T(8,128)S(1)}) fusion(f32[128,128]{1,0:T(8,128)S(1)} %fusion.53, f32[16]{0:T(128)S(1)} %get-tuple-element.249, f32[16]{0:T(128)S(1)} %get-tuple-element.250, f32[16,128]{1,0:T(8,128)S(1)} %bitcast.104, f32[128]{0:T(128)S(1)} %get-tuple-element.253, f32[16,128]{1,0:T(8,128)S(1)} %bitcast.105, ...), kind=kLoop, calls=%fused_computation.33.clone.1 | loop fusion | flops 15990782 | bytes 2197644 | tf_op jit(solution)/shard_map/while/body/eval_jaxpr/reduce_sum | solution.py:78
  91.1 0.8 dynamic_update_slice.25
  91.9 0.8 dynamic_update_slice.26
  97.1 0.7 compare_convert_fusion.3
  98.9 3.8 %fusion.57 = (f32[]{:T(128)}, f32[]{:T(128)}, f32[16,128,128]{2,1,0:T(8,128)S(1)}) fusion(f32[128,128]{1,0:T(8,128)S(1)} %fusion.53, f32[16]{0:T(128)S(1)} %get-tuple-element.249, f32[16]{0:T(128)S(1)} %get-tuple-element.250, f32[16,128]{1,0:T(8,128)S(1)} %bitcast.104, f32[128]{0:T(128)S(1)} %get-tuple-element.253, f32[16,128]{1,0:T(8,128)S(1)} %bitcast.105, ...), kind=kLoop, calls=%fused_computation.33.clone.1 | loop fusion | flops 15990782 | bytes 2197644 | tf_op jit(solution)/shard_map/while/body/eval_jaxpr/reduce_sum | solution.py:78
  103.2 0.8 dynamic_update_slice.25
  104.0 0.8 dynamic_update_slice.26
  109.2 0.7 compare_convert_fusion.3
  111.1 3.8 %fusion.57 = (f32[]{:T(128)}, f32[]{:T(128)}, f32[16,128,128]{2,1,0:T(8,128)S(1)}) fusion(f32[128,128]{1,0:T(8,128)S(1)} %fusion.53, f32[16]{0:T(128)S(1)} %get-tuple-element.249, f32[16]{0:T(128)S(1)} %get-tuple-element.250, f32[16,128]{1,0:T(8,128)S(1)} %bitcast.104, f32[128]{0:T(128)S(1)} %get-tuple-element.253, f32[16,128]{1,0:T(8,128)S(1)} %bitcast.105, ...), kind=kLoop, calls=%fused_computation.33.clone.1 | loop fusion | flops 15990782 | bytes 2197644 | tf_op jit(solution)/shard_map/while/body/eval_jaxpr/reduce_sum | solution.py:78
  115.4 0.8 dynamic_update_slice.25
  116.1 0.8 dynamic_update_slice.26
  116.9 0.6 reduce_sum.96
  117.5 0.6 reduce_sum.97
  118.1 0.6 reshape.290
  118.7 31.8 %all-reduce = (f32[]{:T(128)}, f32[]{:T(128)}) all-reduce(f32[]{:T(128)} %reduce_sum.96, f32[]{:T(128)} %reduce_sum.97), channel_id=1, replica_groups=mesh['win'=2,'dx'=4,'dy'=2,'dz'=2] {'dx','dy','dz'}, use_global_device_ids=true, to_apply=%region_12.13 | all-reduce | flops 2 | bytes 16 | tf_op jit(solution)/shard_map/psum | solution.py:171
  (127 shorter events, 19.7 us)
Async XLA Ops:
  0.6 12.2 %copy-start.2 = (f32[7]{0:T(128)S(1)}, f32[7]{0:T(128)}, u32[]{:S(2)}) copy-start(f32[7]{0:T(128)} %constant.159.clone.1) | copy-start | bytes 88
  5.1 6.8 %collective-permute-start = (f32[7,16]{0,1:T(8,128)S(1)}, f32[7,16]{0,1:T(8,128)S(1)}, u32[]{:S(2)}, u32[]{:S(2)}) collective-permute-start(f32[7,16]{0,1:T(8,128)S(1)} %bitcast.113), channel_id=1, source_target_pairs={{0,4},{4,8},{8,12},{12,0},{1,5},{5,9},{9,13},{13,1},{2,6},{6,10},{... | collective-permute-start | bytes 1352 | tf_op jit(solution)/shard_map/ppermute | solution.py:15
  8.8 27.1 %copy-start.1 = (s32[1,1,1,6,16]{4,2,3,1,0:T(1,128)S(1)}, s32[1,1,1,6,16]{4,2,3,1,0:T(1,128)}, u32[]{:S(2)}) copy-start(s32[1,1,1,6,16]{4,2,3,1,0:T(1,128)} %param.19) | copy-start | bytes 1156
  8.8 4.0 %collective-permute-start.1 = (f32[7,16]{0,1:T(8,128)S(1)}, f32[7,16]{0,1:T(8,128)S(1)}, u32[]{:S(2)}, u32[]{:S(2)}) collective-permute-start(f32[7,16]{0,1:T(8,128)S(1)} %bitcast.112), channel_id=1, source_target_pairs={{0,12},{4,0},{8,4},{12,8},{1,13},{5,1},{9,5},{13,9},{2,14},{6,2},{... | collective-permute-start | bytes 1352 | tf_op jit(solution)/shard_map/ppermute | solution.py:15
  12.8 27.1 %copy-start = (f32[3]{0:T(128)S(1)}, f32[3]{0:T(128)}, u32[]{:S(2)}) copy-start(f32[3]{0:T(128)} %param.24) | copy-start | bytes 40
  13.7 13.0 %collective-permute-start.3 = (f32[7,1,1,1,768]{0,4,3,2,1:T(8,128)S(1)}, f32[7,1,1,1,768]{0,4,3,2,1:T(8,128)S(1)}, u32[]{:S(2)}, u32[]{:S(2)}) collective-permute-start(f32[7,1,1,1,768]{0,4,3,2,1:T(8,128)S(1)} %bitcast.97), channel_id=1, source_target_pairs={{4,0},{8,4},{12,8},{0,12},{5,1},{9,5},{13,9},{1,13},{6,2},{10,6},{... | collective-permute-start | bytes 64520 | tf_op jit(solution)/shard_map/ppermute | solution.py:27
  17.2 16.4 %collective-permute-start.2 = (f32[7,1,1,1,768]{0,4,3,2,1:T(8,128)S(1)}, f32[7,1,1,1,768]{0,4,3,2,1:T(8,128)S(1)}, u32[]{:S(2)}, u32[]{:S(2)}) collective-permute-start(f32[7,1,1,1,768]{0,4,3,2,1:T(8,128)S(1)} %bitcast.98), channel_id=1, source_target_pairs={{0,4},{4,8},{8,12},{12,0},{1,5},{5,9},{9,13},{13,1},{2,6},{6,10},{... | collective-permute-start | bytes 64520 | tf_op jit(solution)/shard_map/ppermute | solution.py:24
  33.9 4.3 %collective-permute-start.5 = (f32[7,3,1,1,768]{4,3,2,1,0:T(1,128)S(1)}, f32[7,3,1,1,768]{4,3,2,1,0:T(1,128)S(1)}, u32[]{:S(2)}, u32[]{:S(2)}) collective-permute-start(f32[7,3,1,1,768]{4,3,2,1,0:T(1,128)S(1)} %pad_maximum_fusion.2), channel_id=1, source_target_pairs={{2,0},{0,2},{3,1},{1,3},{6,4},{4,6},{7,5},{5,7},{10,8},{8,10},{11,... | collective-permute-start | bytes 193544 | tf_op jit(solution)/shard_map/ppermute | solution.py:27
  35.4 4.3 %collective-permute-start.4 = (f32[7,3,1,1,768]{4,3,2,1,0:T(1,128)S(1)}, f32[7,3,1,1,768]{4,3,2,1,0:T(1,128)S(1)}, u32[]{:S(2)}, u32[]{:S(2)}) collective-permute-start(f32[7,3,1,1,768]{4,3,2,1,0:T(1,128)S(1)} %pad_maximum_fusion.2), channel_id=1, source_target_pairs={{0,2},{2,0},{1,3},{3,1},{4,6},{6,4},{5,7},{7,5},{8,10},{10,8},{9,1... | collective-permute-start | bytes 193544 | tf_op jit(solution)/shard_map/ppermute | solution.py:24
  39.8 1.5 collective-permute-start.6
  41.5 2.7 %copy-start.3 = (s32[1,1,1,6]{3,2,1,0:T(1,128)S(1)}, s32[1,1,1,6]{3,2,1,0:T(1,128)}, u32[]{:S(2)}) copy-start(s32[1,1,1,6]{3,2,1,0:T(1,128)} %param.20) | copy-start | bytes 76
where the time goes:
time: 155 us; the launch traced here: 154 us
  other arithmetic  41.6 us (27%)
  blocking collectives  31.8 us (21%)
  local copies, waits for them, and re-layouts  23.9 us (15%)
  waiting for transfers between devices  21.5 us (14%)
  loops' own time  20 us (13%)
  starting transfers between devices  10.9 us (7%)
  between operations  4.44 us (3%)
    psum x1, blocking collectives, on_device(): lax.psum((jnp.sum(energies), jnp.sum(dhdls)), ('dx', 'dy', 'dz'))  31.8 us
    reduce_sum x6, other arithmetic, pair_block(): jnp.sum(flagged * (-total_pair + weight * (grad_six * sigma_six * soft_al...  23.1 us
    another operation x1, loops' own time, on_device(): lax.map(one_block, jnp.arange(block_total, dtype=jnp.int32))  20 us
    ppermute x2, waiting for transfers between devices, extended(): lax.ppermute(lax.slice_in_dim(block, 0, width, axis=dim), axis, backward)  11.6 us
    dynamic_update_slice x18, local copies, waits for them, and re-layouts, on_device(): lax.map(one_block, jnp.arange(block_total, dtype=jnp.int32))  9.16 us
    ppermute x2, waiting for transfers between devices, extended(): lax.ppermute(lax.slice_in_dim(block, block.shape[dim] - width, None, axis...  8.23 us
    ppermute x2, starting transfers between devices, passed_along(): lax.ppermute(array, axis, [(i, (i + by) % devices) for i in range(devices)])  5.2 us
    ppermute x2, starting transfers between devices, extended(): lax.ppermute(lax.slice_in_dim(block, 0, width, axis=dim), axis, backward)  5.1 us
  transfers between devices with their start and end apart: 7, of which 6 were waited for; matrix products, arithmetic and copies ran while one was open for 2% of the time, Pallas kernels for 0%

commit v1 on v0

--- a/solution.py
+++ b/solution.py
@@ -168,7 +168,9 @@
 
     forces, energies, dhdls = lax.map(one_block, jnp.arange(block_total, dtype=jnp.int32))
     forces = forces.transpose(1, 0, 2).reshape(3, 1, 1, 1, atom_count)
-    window_energy, window_dhdl = lax.psum((jnp.sum(energies), jnp.sum(dhdls)), ("dx", "dy", "dz"))
+    window_energy, window_dhdl = lax.psum(
+        lax.psum((jnp.sum(energies), jnp.sum(dhdls)), ("dy", "dz")), "dx"
+    )
     slot_total = jnp.float32(
         atom_count * lax.axis_size("dx") * lax.axis_size("dy") * lax.axis_size("dz")
     )

time: 155 us -> 141 us (0.910)
  blocking collectives: 31.8 us -> 17.5 us
    psum x1 -> x2, blocking collectives: 31.8 us -> 17.5 us  [the longest x1 10.9 us: on_device(): lax.psum(lax.psum((jnp.sum(energies), jnp.sum(dhdls)), ('dy', 'dz')), 'dx')]
where the time goes in v1:
time: 141 us; the launch traced here: 140 us
  other arithmetic  41.6 us (30%)
  local copies, waits for them, and re-layouts  23.9 us (17%)
  waiting for transfers between devices  21.5 us (15%)
  loops' own time  20 us (14%)
  blocking collectives  17.5 us (12%)
  starting transfers between devices  10.9 us (8%)
  between operations  4.44 us (3%)
    reduce_sum x6, other arithmetic, pair_block(): jnp.sum(flagged * (-total_pair + weight * (grad_six * sigma_six * soft_al...  23.1 us
    another operation x1, loops' own time, on_device(): lax.map(one_block, jnp.arange(block_total, dtype=jnp.int32))  20 us
    ppermute x2, waiting for transfers between devices, extended(): lax.ppermute(lax.slice_in_dim(block, 0, width, axis=dim), axis, backward)  11.6 us
    psum x1, blocking collectives, on_device(): lax.psum(lax.psum((jnp.sum(energies), jnp.sum(dhdls)), ('dy', 'dz')), 'dx')  10.9 us
    dynamic_update_slice x18, local copies, waits for them, and re-layouts, on_device(): lax.map(one_block, jnp.arange(block_total, dtype=jnp.int32))  9.16 us
    ppermute x2, waiting for transfers between devices, extended(): lax.ppermute(lax.slice_in_dim(block, block.shape[dim] - width, None, axis...  8.23 us
    psum x1, blocking collectives, on_device(): lax.psum((jnp.sum(energies), jnp.sum(dhdls)), ('dy', 'dz'))  6.69 us
    ppermute x2, starting transfers between devices, passed_along(): lax.ppermute(array, axis, [(i, (i + by) % devices) for i in range(devices)])  5.2 us
  transfers between devices with their start and end apart: 7, of which 6 were waited for; matrix products, arithmetic and copies ran while one was open for 2% of the time, Pallas kernels for 0%

profile of v1, /device:TPU:0, one launch (start us, length us, event | category | flops | bytes accessed | tf_op | source)
XLA Modules:
  0.0 139.8 jit_solution(1080846883325533464)
XLA Ops:
  0.6 0.8 fusion.44
  1.4 0.7 convert_bitcast_fusion
  2.1 0.7 reduce.2
  2.8 0.8 select_reduce_fusion
  3.6 0.7 copy.79
  5.1 3.1 %collective-permute-start = (f32[7,16]{0,1:T(8,128)S(1)}, f32[7,16]{0,1:T(8,128)S(1)}, u32[]{:S(2)}, u32[]{:S(2)}) collective-permute-start(f32[7,16]{0,1:T(8,128)S(1)} %bitcast.113), channel_id=1, source_target_pairs={{0,4},{4,8},{8,12},{12,0},{1,5},{5,9},{9,13},{13,1},{2,6},{6,10},{... | collective-permute-start | bytes 1352 | tf_op jit(solution)/shard_map/ppermute | solution.py:15
  8.8 2.1 %collective-permute-start.1 = (f32[7,16]{0,1:T(8,128)S(1)}, f32[7,16]{0,1:T(8,128)S(1)}, u32[]{:S(2)}, u32[]{:S(2)}) collective-permute-start(f32[7,16]{0,1:T(8,128)S(1)} %bitcast.112), channel_id=1, source_target_pairs={{0,12},{4,0},{8,4},{12,8},{1,13},{5,1},{9,5},{13,9},{2,14},{6,2},{... | collective-permute-start | bytes 1352 | tf_op jit(solution)/shard_map/ppermute | solution.py:15
  10.9 1.0 collective-permute-done
  11.9 0.9 scatter_custom_fusion
  12.9 0.8 scatter_custom_fusion.1
  13.7 3.5 %collective-permute-start.3 = (f32[7,1,1,1,768]{0,4,3,2,1:T(8,128)S(1)}, f32[7,1,1,1,768]{0,4,3,2,1:T(8,128)S(1)}, u32[]{:S(2)}, u32[]{:S(2)}) collective-permute-start(f32[7,1,1,1,768]{0,4,3,2,1:T(8,128)S(1)} %bitcast.97), channel_id=1, source_target_pairs={{4,0},{8,4},{12,8},{0,12},{5,1},{9,5},{13,9},{1,13},{6,2},{10,6},{... | collective-permute-start | bytes 64520 | tf_op jit(solution)/shard_map/ppermute | solution.py:27
  17.4 9.4 %collective-permute-done.3 = f32[7,1,1,1,768]{0,4,3,2,1:T(8,128)S(1)} collective-permute-done((f32[7,1,1,1,768]{0,4,3,2,1:T(8,128)S(1)}, f32[7,1,1,1,768]{0,4,3,2,1:T(8,128)S(1)}, u32[]{:S(2)}, u32[]{:S(2)}) %collective-permute-start.3) | collective-permute-done | bytes 21536 | tf_op jit(solution)/shard_map/ppermute | solution.py:27
  26.9 6.7 %collective-permute-done.2 = f32[7,1,1,1,768]{0,4,3,2,1:T(8,128)S(1)} collective-permute-done((f32[7,1,1,1,768]{0,4,3,2,1:T(8,128)S(1)}, f32[7,1,1,1,768]{0,4,3,2,1:T(8,128)S(1)}, u32[]{:S(2)}, u32[]{:S(2)}) %collective-permute-start.2) | collective-permute-done | bytes 21536 | tf_op jit(solution)/shard_map/ppermute | solution.py:24
  33.9 1.6 %collective-permute-start.5 = (f32[7,3,1,1,768]{4,3,2,1,0:T(1,128)S(1)}, f32[7,3,1,1,768]{4,3,2,1,0:T(1,128)S(1)}, u32[]{:S(2)}, u32[]{:S(2)}) collective-permute-start(f32[7,3,1,1,768]{4,3,2,1,0:T(1,128)S(1)} %pad_maximum_fusion.2), channel_id=1, source_target_pairs={{2,0},{0,2},{3,1},{1,3},{6,4},{4,6},{7,5},{5,7},{10,8},{8,10},{11,... | collective-permute-start | bytes 193544 | tf_op jit(solution)/shard_map/ppermute | solution.py:27
  36.0 2.2 %collective-permute-done.5 = f32[7,3,1,1,768]{4,3,2,1,0:T(1,128)S(1)} collective-permute-done((f32[7,3,1,1,768]{4,3,2,1,0:T(1,128)S(1)}, f32[7,3,1,1,768]{4,3,2,1,0:T(1,128)S(1)}, u32[]{:S(2)}, u32[]{:S(2)}) %collective-permute-start.5) | collective-permute-done | bytes 64544 | tf_op jit(solution)/shard_map/ppermute | solution.py:27
  38.2 1.5 %collective-permute-done.4 = f32[7,3,1,1,768]{4,3,2,1,0:T(1,128)S(1)} collective-permute-done((f32[7,3,1,1,768]{4,3,2,1,0:T(1,128)S(1)}, f32[7,3,1,1,768]{4,3,2,1,0:T(1,128)S(1)}, u32[]{:S(2)}, u32[]{:S(2)}) %collective-permute-start.4) | collective-permute-done | bytes 64544 | tf_op jit(solution)/shard_map/ppermute | solution.py:24
  39.9 0.7 fusion.46
  40.6 0.7 collective-permute-done.6
  41.5 2.3 %fusion.34 = (f32[1,3,3,3,768]{4,0,3,2,1:T(1,128)S(1)}, f32[1,3,3,3,768]{4,0,3,2,1:T(1,128)S(1)}, f32[1,3,3,3,768]{4,0,3,2,1:T(1,128)S(1)}) fusion(f32[7,3,3,3,768]{4,0,3,2,1:T(8,128)S(1)} %copy_dynamic-update-slice_fusion.1, f32[3]{0:T(128)S(1)} %iota_add_fusion, f32[]{:T(128)} %bitcast.28, f32[]{:T(128)} %bitcast.32, f32[]{:T(128)} %bitcast.30), kind=kLoop, calls=%fused_computation.81 | loop fusion | flops 186624 | bytes 499212 | tf_op jit(solution)/shard_map/mul | solution.py:143
  44.2 72.7 %while.17 = (s32[]{:T(128)}, f32[6,3,128]{2,1,0:T(4,128)S(1)}, f32[6]{0:T(128)S(1)}, f32[6]{0:T(128)S(1)}, f32[]{:T(128)}, /*index=5*/s32[6]{0:T(128)S(1)}, f32[...) while((s32[]{:T(128)}, f32[6,3,128]{2,1,0:T(4,128)S(1)}, ...), condition=%wide.region_10.11_spmd, body=%wide.region_5.10_spmd.sunk | while | flops 20495192 | bytes 4781457 | solution.py:169
  48.6 0.7 compare_convert_fusion.3
  50.5 3.8 %fusion.57 = (f32[]{:T(128)}, f32[]{:T(128)}, f32[16,128,128]{2,1,0:T(8,128)S(1)}) fusion(f32[128,128]{1,0:T(8,128)S(1)} %fusion.53, f32[16]{0:T(128)S(1)} %get-tuple-element.251, f32[16]{0:T(128)S(1)} %get-tuple-element.252, f32[16,128]{1,0:T(8,128)S(1)} %bitcast.104, f32[128]{0:T(128)S(1)} %get-tuple-element.255, f32[16,128]{1,0:T(8,128)S(1)} %bitcast.105, ...), kind=kLoop, calls=%fused_computation.33.clone.1 | loop fusion | flops 15990782 | bytes 2197644 | tf_op jit(solution)/shard_map/while/body/eval_jaxpr/reduce_sum | solution.py:78
  54.8 0.8 dynamic_update_slice.25
  55.6 0.8 dynamic_update_slice.26
  60.8 0.7 compare_convert_fusion.3
  62.6 3.8 %fusion.57 = (f32[]{:T(128)}, f32[]{:T(128)}, f32[16,128,128]{2,1,0:T(8,128)S(1)}) fusion(f32[128,128]{1,0:T(8,128)S(1)} %fusion.53, f32[16]{0:T(128)S(1)} %get-tuple-element.251, f32[16]{0:T(128)S(1)} %get-tuple-element.252, f32[16,128]{1,0:T(8,128)S(1)} %bitcast.104, f32[128]{0:T(128)S(1)} %get-tuple-element.255, f32[16,128]{1,0:T(8,128)S(1)} %bitcast.105, ...), kind=kLoop, calls=%fused_computation.33.clone.1 | loop fusion | flops 15990782 | bytes 2197644 | tf_op jit(solution)/shard_map/while/body/eval_jaxpr/reduce_sum | solution.py:78
  66.9 0.8 dynamic_update_slice.25
  67.7 0.8 dynamic_update_slice.26
  72.9 0.7 compare_convert_fusion.3
  74.7 3.8 %fusion.57 = (f32[]{:T(128)}, f32[]{:T(128)}, f32[16,128,128]{2,1,0:T(8,128)S(1)}) fusion(f32[128,128]{1,0:T(8,128)S(1)} %fusion.53, f32[16]{0:T(128)S(1)} %get-tuple-element.251, f32[16]{0:T(128)S(1)} %get-tuple-element.252, f32[16,128]{1,0:T(8,128)S(1)} %bitcast.104, f32[128]{0:T(128)S(1)} %get-tuple-element.255, f32[16,128]{1,0:T(8,128)S(1)} %bitcast.105, ...), kind=kLoop, calls=%fused_computation.33.clone.1 | loop fusion | flops 15990782 | bytes 2197644 | tf_op jit(solution)/shard_map/while/body/eval_jaxpr/reduce_sum | solution.py:78
  79.0 0.8 dynamic_update_slice.25
  79.8 0.8 dynamic_update_slice.26
  85.0 0.7 compare_convert_fusion.3
  86.8 3.8 %fusion.57 = (f32[]{:T(128)}, f32[]{:T(128)}, f32[16,128,128]{2,1,0:T(8,128)S(1)}) fusion(f32[128,128]{1,0:T(8,128)S(1)} %fusion.53, f32[16]{0:T(128)S(1)} %get-tuple-element.251, f32[16]{0:T(128)S(1)} %get-tuple-element.252, f32[16,128]{1,0:T(8,128)S(1)} %bitcast.104, f32[128]{0:T(128)S(1)} %get-tuple-element.255, f32[16,128]{1,0:T(8,128)S(1)} %bitcast.105, ...), kind=kLoop, calls=%fused_computation.33.clone.1 | loop fusion | flops 15990782 | bytes 2197644 | tf_op jit(solution)/shard_map/while/body/eval_jaxpr/reduce_sum | solution.py:78
  91.1 0.8 dynamic_update_slice.25
  91.9 0.8 dynamic_update_slice.26
  97.1 0.7 compare_convert_fusion.3
  98.9 3.8 %fusion.57 = (f32[]{:T(128)}, f32[]{:T(128)}, f32[16,128,128]{2,1,0:T(8,128)S(1)}) fusion(f32[128,128]{1,0:T(8,128)S(1)} %fusion.53, f32[16]{0:T(128)S(1)} %get-tuple-element.251, f32[16]{0:T(128)S(1)} %get-tuple-element.252, f32[16,128]{1,0:T(8,128)S(1)} %bitcast.104, f32[128]{0:T(128)S(1)} %get-tuple-element.255, f32[16,128]{1,0:T(8,128)S(1)} %bitcast.105, ...), kind=kLoop, calls=%fused_computation.33.clone.1 | loop fusion | flops 15990782 | bytes 2197644 | tf_op jit(solution)/shard_map/while/body/eval_jaxpr/reduce_sum | solution.py:78
  103.2 0.8 dynamic_update_slice.25
  104.0 0.8 dynamic_update_slice.26
  109.2 0.7 compare_convert_fusion.3
  111.1 3.8 %fusion.57 = (f32[]{:T(128)}, f32[]{:T(128)}, f32[16,128,128]{2,1,0:T(8,128)S(1)}) fusion(f32[128,128]{1,0:T(8,128)S(1)} %fusion.53, f32[16]{0:T(128)S(1)} %get-tuple-element.251, f32[16]{0:T(128)S(1)} %get-tuple-element.252, f32[16,128]{1,0:T(8,128)S(1)} %bitcast.104, f32[128]{0:T(128)S(1)} %get-tuple-element.255, f32[16,128]{1,0:T(8,128)S(1)} %bitcast.105, ...), kind=kLoop, calls=%fused_computation.33.clone.1 | loop fusion | flops 15990782 | bytes 2197644 | tf_op jit(solution)/shard_map/while/body/eval_jaxpr/reduce_sum | solution.py:78
  115.4 0.8 dynamic_update_slice.25
  116.1 0.8 dynamic_update_slice.26
  116.9 0.6 reduce_sum.96
  118.1 0.6 reshape.290
  118.7 6.7 %all-reduce = (f32[]{:T(128)}, f32[]{:T(128)}) all-reduce(f32[]{:T(128)} %reduce_sum.96, f32[]{:T(128)} %reduce_sum.97), channel_id=1, replica_groups=mesh['win'=2,'dx'=4,'dy'=2,'dz'=2] {'dy','dz'}, use_global_device_ids=true, to_apply=%region_12.13 | all-reduce | flops 2 | bytes 16 | tf_op jit(solution)/shard_map/psum | solution.py:172
  125.4 10.9 %all-reduce.1 = (f32[]{:T(128)}, f32[]{:T(128)}) all-reduce(f32[]{:T(128)} %get-tuple-element.156, f32[]{:T(128)} %get-tuple-element.157), channel_id=1, replica_groups=mesh['win'=2,'dx'=4,'dy'=2,'dz'=2] {'dx'}, use_global_device_ids=true, to_apply=%region_13.14 | all-reduce | flops 2 | bytes 16 | tf_op jit(solution)/shard_map/psum | solution.py:171
  (128 shorter events, 20.3 us)
Async XLA Ops:
  0.6 12.2 %copy-start.2 = (f32[7]{0:T(128)S(1)}, f32[7]{0:T(128)}, u32[]{:S(2)}) copy-start(f32[7]{0:T(128)} %constant.159.clone.1) | copy-start | bytes 88
  5.1 6.8 %collective-permute-start = (f32[7,16]{0,1:T(8,128)S(1)}, f32[7,16]{0,1:T(8,128)S(1)}, u32[]{:S(2)}, u32[]{:S(2)}) collective-permute-start(f32[7,16]{0,1:T(8,128)S(1)} %bitcast.113), channel_id=1, source_target_pairs={{0,4},{4,8},{8,12},{12,0},{1,5},{5,9},{9,13},{13,1},{2,6},{6,10},{... | collective-permute-start | bytes 1352 | tf_op jit(solution)/shard_map/ppermute | solution.py:15
  8.8 27.1 %copy-start.1 = (s32[1,1,1,6,16]{4,2,3,1,0:T(1,128)S(1)}, s32[1,1,1,6,16]{4,2,3,1,0:T(1,128)}, u32[]{:S(2)}) copy-start(s32[1,1,1,6,16]{4,2,3,1,0:T(1,128)} %param.19) | copy-start | bytes 1156
  8.8 4.0 %collective-permute-start.1 = (f32[7,16]{0,1:T(8,128)S(1)}, f32[7,16]{0,1:T(8,128)S(1)}, u32[]{:S(2)}, u32[]{:S(2)}) collective-permute-start(f32[7,16]{0,1:T(8,128)S(1)} %bitcast.112), channel_id=1, source_target_pairs={{0,12},{4,0},{8,4},{12,8},{1,13},{5,1},{9,5},{13,9},{2,14},{6,2},{... | collective-permute-start | bytes 1352 | tf_op jit(solution)/shard_map/ppermute | solution.py:15
  12.8 27.1 %copy-start = (f32[3]{0:T(128)S(1)}, f32[3]{0:T(128)}, u32[]{:S(2)}) copy-start(f32[3]{0:T(128)} %param.24) | copy-start | bytes 40
  13.7 13.0 %collective-permute-start.3 = (f32[7,1,1,1,768]{0,4,3,2,1:T(8,128)S(1)}, f32[7,1,1,1,768]{0,4,3,2,1:T(8,128)S(1)}, u32[]{:S(2)}, u32[]{:S(2)}) collective-permute-start(f32[7,1,1,1,768]{0,4,3,2,1:T(8,128)S(1)} %bitcast.97), channel_id=1, source_target_pairs={{4,0},{8,4},{12,8},{0,12},{5,1},{9,5},{13,9},{1,13},{6,2},{10,6},{... | collective-permute-start | bytes 64520 | tf_op jit(solution)/shard_map/ppermute | solution.py:27
  17.2 16.4 %collective-permute-start.2 = (f32[7,1,1,1,768]{0,4,3,2,1:T(8,128)S(1)}, f32[7,1,1,1,768]{0,4,3,2,1:T(8,128)S(1)}, u32[]{:S(2)}, u32[]{:S(2)}) collective-permute-start(f32[7,1,1,1,768]{0,4,3,2,1:T(8,128)S(1)} %bitcast.98), channel_id=1, source_target_pairs={{0,4},{4,8},{8,12},{12,0},{1,5},{5,9},{9,13},{13,1},{2,6},{6,10},{... | collective-permute-start | bytes 64520 | tf_op jit(solution)/shard_map/ppermute | solution.py:24
  33.9 4.3 %collective-permute-start.5 = (f32[7,3,1,1,768]{4,3,2,1,0:T(1,128)S(1)}, f32[7,3,1,1,768]{4,3,2,1,0:T(1,128)S(1)}, u32[]{:S(2)}, u32[]{:S(2)}) collective-permute-start(f32[7,3,1,1,768]{4,3,2,1,0:T(1,128)S(1)} %pad_maximum_fusion.2), channel_id=1, source_target_pairs={{2,0},{0,2},{3,1},{1,3},{6,4},{4,6},{7,5},{5,7},{10,8},{8,10},{11,... | collective-permute-start | bytes 193544 | tf_op jit(solution)/shard_map/ppermute | solution.py:27
  35.4 4.3 %collective-permute-start.4 = (f32[7,3,1,1,768]{4,3,2,1,0:T(1,128)S(1)}, f32[7,3,1,1,768]{4,3,2,1,0:T(1,128)S(1)}, u32[]{:S(2)}, u32[]{:S(2)}) collective-permute-start(f32[7,3,1,1,768]{4,3,2,1,0:T(1,128)S(1)} %pad_maximum_fusion.2), channel_id=1, source_target_pairs={{0,2},{2,0},{1,3},{3,1},{4,6},{6,4},{5,7},{7,5},{8,10},{10,8},{9,1... | collective-permute-start | bytes 193544 | tf_op jit(solution)/shard_map/ppermute | solution.py:24
  39.8 1.5 %collective-permute-start.6 = (f32[7,3,3,1,768]{4,3,2,1,0:T(1,128)S(1)}, f32[7,3,3,1,768]{4,3,2,1,0:T(1,128)S(1)}, u32[]{:S(2)}, u32[]{:S(2)}) collective-permute-start(f32[7,3,3,1,768]{4,3,2,1,0:T(1,128)S(1)} %pad_maximum_fusion.1), channel_id=1, source_target_pairs={{0,1},{1,0},{2,3},{3,2},{4,5},{5,4},{6,7},{7,6},{8,9},{9,8},{10,11... | collective-permute-start | bytes 580616 | tf_op jit(solution)/shard_map/ppermute | solution.py:39
  41.5 2.7 %copy-start.3 = (s32[1,1,1,6]{3,2,1,0:T(1,128)S(1)}, s32[1,1,1,6]{3,2,1,0:T(1,128)}, u32[]{:S(2)}) copy-start(s32[1,1,1,6]{3,2,1,0:T(1,128)} %param.20) | copy-start | bytes 76
